TPU v7x, 16 devices: a whole 2x2x2 slice. The times are simulated.
16 devices in a mesh: dp: 1, tp: 16 (over x, y, z, core).
Axes of the slice: x: 2, y: 2, z: 2, core: 2. Of those that a mesh axis runs over, the one named last changes fastest.
Arguments:
- x: bfloat16 [64, 3072], P('dp')
- k_cache: bfloat16 [64, 4096, 32, 96], P('dp', None, 'tp')
- v_cache: bfloat16 [64, 4096, 32, 96], P('dp', None, 'tp')
- gain_a: bfloat16 [3072], replicated
- wq: bfloat16 [3072, 3072], P(None, 'tp')
- wo: bfloat16 [3072, 3072], P('tp')
- gain_m: bfloat16 [3072], replicated
- w_gate: bfloat16 [3072, 8192], P(None, 'tp')
- w_up: bfloat16 [3072, 8192], P(None, 'tp')
- w_down: bfloat16 [8192, 3072], P('tp')
Outputs:
- output: bfloat16 [64, 3072], P('dp')
All inputs are finite; a program needn't handle non-finite values.
Results may differ from a plain program's by a relative error of at most 0.017.
Values are sent between devices in bfloat16 or wider.
A program may use at most 2 GiB of HBM per device.

v0:
```python
import jax
import jax.numpy as jnp
from jax import lax
from jax.sharding import PartitionSpec as P

HEAD = 96
THETA = 10000


def normed(x, gain):
    wide = x.astype(jnp.float32)
    scale = lax.rsqrt(jnp.mean(wide * wide, -1, keepdims=True) + 1e-6)
    return (wide * scale * gain.astype(jnp.float32)).astype(jnp.bfloat16)


def turned(t, place, theta):
    half = t.shape[-1] // 2
    angle = place.astype(jnp.float32)[:, None] * theta ** (-jnp.arange(half, dtype=jnp.float32) / half)
    cos, sin = jnp.cos(angle)[:, None], jnp.sin(angle)[:, None]
    a, b = t[..., :half].astype(jnp.float32), t[..., half:].astype(jnp.float32)
    return jnp.concatenate([a * cos - b * sin, b * cos + a * sin], -1).astype(jnp.bfloat16)


def matmul(a, w):
    return jnp.dot(a, w, preferred_element_type=jnp.float32).astype(jnp.bfloat16)


def einsum(form, a, b):
    return jnp.einsum(form, a.astype(jnp.float32), b.astype(jnp.float32))


def seen_by(a, wq, k_cache, v_cache, head, theta):
    batch, cache, kv_heads = k_cache.shape[:3]
    place = jnp.full((batch,), cache - 1)
    q = turned(matmul(a, wq).reshape(batch, -1, head), place, theta).reshape(batch, kv_heads, -1, head)
    scores = einsum("bgsd,bugd->bgsu", q, k_cache) * head**-0.5
    weights = jax.nn.softmax(scores, -1).astype(jnp.bfloat16)
    return einsum("bgsu,bugd->bgsd", weights, v_cache).astype(jnp.bfloat16).reshape(batch, -1)


def hidden_of(b, w_gate, w_up):
    gate = jnp.dot(b, w_gate, preferred_element_type=jnp.float32)
    up = jnp.dot(b, w_up, preferred_element_type=jnp.float32)
    return (jax.nn.silu(gate) * up).astype(jnp.bfloat16)


def solution(mesh):
    def added(t, term):
        return (t.astype(jnp.float32) + lax.psum(term.astype(jnp.bfloat16), "tp").astype(jnp.float32)).astype(jnp.bfloat16)

    def step(x, k_cache, v_cache, gain_a, wq, wo, gain_m, w_gate, w_up, w_down):
        seen = seen_by(normed(x, gain_a), wq, k_cache, v_cache, HEAD, THETA)
        h = added(x, jnp.dot(seen, wo, preferred_element_type=jnp.float32))
        return added(h, jnp.dot(hidden_of(normed(h, gain_m), w_gate, w_up), w_down, preferred_element_type=jnp.float32))

    states, cache, columns, rows_of = P("dp", None), P("dp", None, "tp", None), P(None, "tp"), P("tp", None)
    return jax.shard_map(
        step,
        mesh=mesh,
        in_specs=(states, cache, cache, P(None), columns, rows_of, P(None), columns, columns, rows_of),
        out_specs=states,
        check_vma=False,
    )
```

profile of v0, /device:TPU:0, one launch (start us, length us, event | category | flops | bytes accessed | tf_op | source)
XLA Modules:
  0.0 239.3 jit_solution(1357968965593806098)
XLA Ops:
  6.5 0.0 copy-start
  6.5 0.0 all-reduce.3.cloned.1.call-start
  6.6 0.8 convert_element_type.66
  7.4 1.2 fusion.12
  8.7 1.9 convolution_convert_fusion.2
  10.6 0.1 copy.11
  10.7 0.1 fusion.34
  10.9 0.1 copy.12
  11.0 34.6 %fusion.45 = f32[64,2,1,4096]{3,2,1,0:T(1,128)} fusion(bf16[64,2,96,1]{2,3,1,0:T(2,128)(2,1)S(1)} %copy.12, bf16[64,4096,2,96]{1,3,2,0:T(8,128)(2,1)} %param.11), kind=kOutput, calls=%fused_computation.58 | convolution fusion | flops 100663296 | bytes 102785024 | tf_op jit(solution)/shard_map/bgsd,bugd->bgsu/dot_general | solution.py:29
  45.6 5.3 %fusion.6 = bf16[64,2,4096,1]{2,0,1,3:T(8,128)(2,1)} fusion(f32[64,2,1,4096]{3,2,1,0:T(1,128)} %fusion.45), kind=kOutput, calls=%fused_computation.6 | output fusion | flops 2105598 | bytes 3145728 | tf_op jit(solution)/shard_map/div | solution.py:37
  50.9 36.2 %fusion.7 = f32[64,2,1,96]{3,2,1,0:T(1,128)S(1)} fusion(bf16[64,4096,2,96]{1,3,2,0:T(8,128)(2,1)} %param.12, bf16[64,2,4096,1]{2,0,1,3:T(8,128)(2,1)} %fusion.6), kind=kOutput, calls=%fused_computation.10 | convolution fusion | flops 100663296 | bytes 101761024 | tf_op jit(solution)/shard_map/bgsu,bugd->bgsd/dot_general | solution.py:29
  87.1 0.0 copy-start.1
  87.2 0.1 reshape.62
  87.2 2.4 convolution_convert_fusion.1
  89.6 0.0 all-reduce.3.cloned.1.call-update
  89.6 0.0 all-reduce.5.cloned.1.call-start
  89.7 0.0 copy-done.1
  89.7 68.3 %all-reduce.3.cloned.1.call-done = bf16[64,3072]{1,0:T(8,128)(2,1)} async-done(((bf16[64,3072]{1,0:T(8,128)(2,1)}), bf16[64,3072]{1,0:T(8,128)(2,1)}) %all-reduce.3.cloned.1.call-update) | async-done | bytes 393232 | tf_op jit(solution)/shard_map/psum | solution.py:49
  158.0 1.4 fusion.16
  159.4 3.2 %fusion.30 = f32[64,512]{1,0:T(8,128)} fusion(bf16[3072,512]{1,0:T(8,128)(2,1)} %param.17, bf16[64,3072]{1,0:T(8,128)(2,1)S(1)} %get-tuple-element.6, f32[3072]{0:T(1024)S(1)} %convert_element_type.77, f32[64]{0:T(128)S(1)} %add_rsqrt_fusion), kind=kOutput, calls=%fused_computation.38 | convolution fusion | flops 202113024 | bytes 3682560 | tf_op jit(solution)/shard_map/dot_general | solution.py:42
  162.6 0.0 copy-done
  162.6 4.0 %convolution_convert_fusion = bf16[64,3072]{1,0:T(8,128)(2,1)} fusion(bf16[512,3072]{1,0:T(8,128)(2,1)S(1)} %copy-done, bf16[3072,512]{1,0:T(8,128)(2,1)} %param.18, f32[64,512]{1,0:T(8,128)} %fusion.30, bf16[64,3072]{1,0:T(8,128)(2,1)S(1)} %get-tuple-element.6, f32[3072]{0:T(1024)S(1)} %convert_element_type.77, f32[64]{0:T(128)S(1)} %add_rsqrt_fusion), kind=kOutput, calls=%fused_computation.7 | convolution fusion | flops 403832832 | bytes 7221504 | tf_op jit(solution)/shard_map/dot_general | solution.py:54
  166.6 0.0 all-reduce.5.cloned.1.call-update
  166.6 64.0 %all-reduce.5.cloned.1.call-done = bf16[64,3072]{1,0:T(8,128)(2,1)} async-done(((bf16[64,3072]{1,0:T(8,128)(2,1)}), bf16[64,3072]{1,0:T(8,128)(2,1)}) %all-reduce.5.cloned.1.call-update) | async-done | bytes 393232 | tf_op jit(solution)/shard_map/psum | solution.py:49
  230.6 1.8 fusion.19
  (6 shorter events, 0.1 us)
Async XLA Ops:
  6.5 156.1 %copy-start = (bf16[512,3072]{1,0:T(8,128)(2,1)S(1)}, bf16[512,3072]{1,0:T(8,128)(2,1)}, u32[]{:S(2)}) copy-start(bf16[512,3072]{1,0:T(8,128)(2,1)} %param.19) | copy-start | bytes 9437188
  6.5 151.5 %all-reduce.3.cloned.1.call-start = ((), (), s32[]{:S(2)}) async-start(), calls=%async_computation | async-start | bytes 786432 | tf_op jit(solution)/shard_map/psum | solution.py:49
  87.1 2.6 %copy-start.1 = (bf16[3072]{0:T(1024)(128)(2,1)S(1)}, bf16[3072]{0:T(1024)(128)(2,1)}, u32[]{:S(2)}) copy-start(bf16[3072]{0:T(1024)(128)(2,1)} %param.16) | copy-start | bytes 18436
  89.6 141.0 %all-reduce.5.cloned.1.call-start = ((), (), s32[]{:S(2)}) async-start(), calls=%async_computation.1 | async-start | bytes 786432 | tf_op jit(solution)/shard_map/psum | solution.py:49
Sparse Core Ops, SparseCore 0:
  89.7 68.2 all-reduce.2
  166.7 63.8 all-reduce.4
where the time goes:
time: 240 us; the launch traced here: 239 us
  waiting for transfers between devices  132 us (55%)
  matrix products  82.3 us (34%)
  between operations  13.5 us (6%)
  other arithmetic  10.8 us (4%)
    psum x2, waiting for transfers between devices, added(): lax.psum(term.astype(jnp.bfloat16), 'tp').astype(jnp.float32)  132 us
    dot_general x2, matrix products, einsum(): return jnp.einsum(form, a.astype(jnp.float32), b.astype(jnp.float32))  70.8 us
    div x1, other arithmetic, seen_by(): weights = jax.nn.softmax(scores, -1).astype(jnp.bfloat16)  5.3 us
  transfers between devices with their start and end apart: 2, of which 2 were waited for; matrix products, arithmetic and copies ran while one was open for 0% of the time, Pallas kernels for 0%

commit v1 on v0

v1 whole, which is shorter than its diff:
```python
import functools

import jax
import jax.numpy as jnp
import numpy as np
from jax import lax
from jax.experimental import pallas as pl
from jax.experimental.pallas import tpu as pltpu
from jax.sharding import PartitionSpec as P

HEAD = 96
THETA = 10000

ROWS = 64
D = 3072
SPAN = 4096
QD = 192
FF = 512
GROUP = 4
GROUPS = ROWS // GROUP
STACK = GROUP * QD
PIECES = 4
PIECE = SPAN // PIECES
SLOTS = 2
CHUNK = 16
CHUNKS = ROWS // CHUNK
PER = CHUNK // GROUP
N = 16
OWN = D // (N // 2)

F32, BF16 = jnp.float32, jnp.bfloat16
NT = (((1,), (1,)), ((), ()))


def dot(a, b):
    return jnp.dot(a, b, preferred_element_type=F32)


def iota(shape, axis):
    return lax.broadcasted_iota(jnp.int32, shape, axis)


def ones_where(keep):
    return jnp.where(keep, 1.0, 0.0).astype(BF16)


def scaled(wide, gain):
    scale = lax.rsqrt(jnp.mean(wide * wide, -1, keepdims=True) + 1e-6)
    return (wide * scale * gain).astype(BF16)


def any_of(d, values):
    found = d == values[0]
    for v in values[1:]:
        found = found | (d == v)
    return found


def kernel(
    x_hbm, k_hbm, v_hbm, turn_ref, gain_a_ref, wq_hbm, wo_hbm, gain_m_ref, wg_hbm, wu_hbm, wd_hbm,
    y_hbm,
    x_v, wq_v, wo_v, wg_v, wu_v, wd_v, k_v, v_v, q_v, s_v, w_v, fold_v, seen_v,
    p1, p2, r1, r2, hb, yb,
    k_sem, v_sem, w_sem, send_sem, recv_sem, out_sem,
):
    me = lax.axis_index("tp")
    my_chip, my_half = me // 2, me % 2
    my_columns = pl.ds(pl.multiple_of(my_chip * OWN, 128), OWN)

    def piece(i):
        return pl.ds(i * PIECE, PIECE)

    def k_copy(g, i):
        slot = lax.rem(g, SLOTS)
        return pltpu.make_async_copy(k_hbm.at[g, :, piece(i)], k_v.at[slot, :, piece(i)], k_sem.at[slot, i])

    def v_copy(g, i):
        slot = lax.rem(g, SLOTS)
        return pltpu.make_async_copy(v_hbm.at[g, :, piece(i)], v_v.at[slot, :, piece(i)], v_sem.at[slot, i])

    early = [pltpu.make_async_copy(x_hbm, x_v, w_sem.at[0]), pltpu.make_async_copy(wq_hbm, wq_v, w_sem.at[1])]
    late = [
        pltpu.make_async_copy(wo_hbm, wo_v, w_sem.at[2]),
        pltpu.make_async_copy(wg_hbm, wg_v, w_sem.at[3]),
        pltpu.make_async_copy(wu_hbm, wu_v, w_sem.at[4]),
        pltpu.make_async_copy(wd_hbm, wd_v, w_sem.at[5]),
    ]
    for copy in early:
        copy.start()
    for g in range(SLOTS):
        for i in range(PIECES):
            k_copy(g, i).start()
        for i in range(PIECES):
            v_copy(g, i).start()
    for copy in late:
        copy.start()

    barrier = pltpu.get_barrier_semaphore()
    for p in range(1, N):
        pl.semaphore_signal(barrier, inc=1, device_id={"tp": lax.rem(me + p, N)}, device_id_type=pl.DeviceIdType.MESH)

    for copy in early:
        copy.wait()
    a = scaled(x_v[...].reshape(ROWS, D).astype(F32), gain_a_ref[...].astype(F32))
    q = lax.dot_general(a, wq_v[...], NT, preferred_element_type=F32).astype(BF16)
    i, j = iota((QD, QD), 0), iota((QD, QD), 1)
    first = (j < 48) | ((j >= 96) & (j < 144))
    swapped = dot(q, ones_where(((i - j == 48) & first) | ((i - j == -48) & ~first)))
    q = (q.astype(F32) * turn_ref[0:1, :] + swapped * turn_ref[1:2, :]).astype(BF16)
    places = [QD * n for n in range(GROUP)]
    spread = ones_where(any_of(iota((QD, STACK), 1) - iota((QD, STACK), 0), places))
    wide = dot(q, spread).astype(BF16)
    i = iota((2 * ROWS, ROWS), 0)
    wide = dot(ones_where((i >> 3) * GROUP + (i & 3) == iota((2 * ROWS, ROWS), 1)), wide)
    r, c = iota((2 * ROWS, STACK), 0), iota((2 * ROWS, STACK), 1)
    low = (r & 3) * QD + ((r >> 2) & 1) * HEAD
    q_v[...] = jnp.where((c >= low) & (c < low + HEAD), wide, 0.0).reshape(GROUPS, 8, STACK)
    fold_v[...] = ones_where(any_of(iota((STACK, QD), 0) - iota((STACK, QD), 1), places))

    def attend(g):
        slot = lax.rem(g, SLOTS)
        queries = q_v[g].astype(BF16)
        for i in range(PIECES):
            k_copy(g, i).wait()
            s_v[:, piece(i)] = dot(queries, k_v[slot, :, piece(i)]) * HEAD**-0.5

            @pl.when(g + SLOTS < GROUPS)
            def _():
                k_copy(g + SLOTS, i).start()

        s = s_v[...]
        e = jnp.exp(s - jnp.max(s, -1, keepdims=True))
        w_v[...] = (e * (1.0 / jnp.sum(e, -1, keepdims=True))).astype(BF16)
        total = jnp.zeros((8, STACK), F32)
        for i in range(PIECES):
            v_copy(g, i).wait()
            total += lax.dot_general(w_v[:, piece(i)], v_v[slot, :, piece(i)], NT, preferred_element_type=F32)

            @pl.when(g + SLOTS < GROUPS)
            def _():
                v_copy(g + SLOTS, i).start()

        r, c = iota((8, STACK), 0), iota((8, STACK), 1)
        low = (r & 3) * QD + (r >> 2) * HEAD
        own = jnp.where((c >= low) & (c < low + HEAD), total, 0.0).astype(BF16)
        seen_v[g] = dot(own, fold_v[...])

    def scatter(phase, chunk, parts, landing):
        @pl.loop(1, N)
        def _(p):
            peer = lax.rem(me + p, N)
            pltpu.make_async_remote_copy(
                src_ref=parts.at[chunk, peer % 2, :, pl.ds(pl.multiple_of(peer // 2 * OWN, 128), OWN)],
                dst_ref=landing.at[chunk, me],
                send_sem=send_sem.at[phase],
                recv_sem=recv_sem.at[phase, chunk],
                device_id={"tp": peer},
                device_id_type=pl.DeviceIdType.MESH,
            ).start()

    def spread_out(phase, chunk, whole):
        block = whole.at[chunk, my_half, :, my_columns]

        @pl.loop(1, N)
        def _(p):
            pltpu.make_async_remote_copy(
                src_ref=block,
                dst_ref=block,
                send_sem=send_sem.at[phase],
                recv_sem=recv_sem.at[phase, chunk],
                device_id={"tp": lax.rem(me + p, N)},
                device_id_type=pl.DeviceIdType.MESH,
            ).start()

    def arrived(phase, chunk):
        pltpu.make_async_copy(r1.at[0, pl.ds(0, N - 1)], r1.at[0, pl.ds(0, N - 1)], recv_sem.at[phase, chunk]).wait()

    def total_of(chunk, parts, landing):
        total = parts[chunk, my_half, :, my_columns].astype(F32)

        def add(p, total):
            return total + landing[chunk, lax.rem(me + p, N)].astype(F32)

        return lax.fori_loop(1, N, add, total, unroll=True)

    def project(chunk):
        rows = seen_v[pl.ds(chunk * PER, PER)].reshape(8 * PER, QD).astype(BF16)
        i, j = iota((CHUNK, 8 * PER), 0), iota((CHUNK, 8 * PER), 1)
        seen = dot(ones_where((j >> 3) * GROUP + (j & 3) == i), rows).astype(BF16)
        term = dot(seen, wo_v[...]).astype(BF16)
        p1[chunk, 0] = term[0:8]
        p1[chunk, 1] = term[8:16]
        scatter(0, chunk, p1, r1)

    def finish_h(chunk):
        arrived(0, chunk)
        x = x_v[chunk * 2 + my_half, :, my_columns].astype(F32)
        hb[chunk, my_half, :, my_columns] = (x + total_of(chunk, p1, r1)).astype(BF16)
        spread_out(1, chunk, hb)

    def mlp(chunk):
        arrived(1, chunk)
        h = hb[chunk].astype(F32).reshape(CHUNK, D)
        b = scaled(h, gain_m_ref[...].astype(F32))
        hidden = (jax.nn.silu(dot(b, wg_v[...])) * dot(b, wu_v[...])).astype(BF16)
        term = dot(hidden, wd_v[...]).astype(BF16)
        p2[chunk, 0] = term[0:8]
        p2[chunk, 1] = term[8:16]
        scatter(2, chunk, p2, r2)

    def finish_y(chunk):
        arrived(2, chunk)
        h = hb[chunk, my_half, :, my_columns].astype(F32)
        yb[chunk, my_half, :, my_columns] = (h + total_of(chunk, p2, r2)).astype(BF16)
        spread_out(3, chunk, yb)

    @pl.loop(0, GROUPS)
    def _(g):
        attend(g)
        chunk, at = g // PER, g % PER

        @pl.when(g == PER - 1)
        def _():
            for copy in late:
                copy.wait()
            pl.semaphore_wait(barrier, N - 1)

        @pl.when(at == PER - 1)
        def _():
            project(chunk)

            @pl.when(chunk >= 1)
            def _():
                mlp(chunk - 1)

        @pl.when((at == 1) & (chunk >= 1))
        def _():
            finish_h(chunk - 1)

            @pl.when(chunk >= 2)
            def _():
                finish_y(chunk - 2)

    last = CHUNKS - 1
    finish_h(last)
    finish_y(last - 1)
    mlp(last)
    finish_y(last)
    for chunk in range(CHUNKS):
        arrived(3, chunk)
    out = pltpu.make_async_copy(yb, y_hbm, out_sem)
    out.start()
    for phase in range(4):
        sent = r1.at[:, pl.ds(0, N - 1)]
        pltpu.make_async_copy(sent, sent, send_sem.at[phase]).wait()
    out.wait()


def turns():
    half = HEAD // 2
    angle = (SPAN - 1) * float(THETA) ** (-np.arange(half) / half)
    cos, sin = np.cos(angle), np.sin(angle)
    table = np.zeros((8, QD), np.float32)
    table[0] = np.tile(np.concatenate([cos, cos]), 2)
    table[1] = np.tile(np.concatenate([-sin, sin]), 2)
    return table


def solution(mesh):
    def step(x, k_cache, v_cache, gain_a, wq, wo, gain_m, w_gate, w_up, w_down):
        hbm = pl.BlockSpec(memory_space=pltpu.HBM)
        vmem = pl.BlockSpec(memory_space=pltpu.VMEM)

        def stacked(cache):
            return cache.transpose(0, 2, 3, 1).reshape(GROUPS, STACK, SPAN)

        y = pl.pallas_call(
            kernel,
            out_shape=jax.ShapeDtypeStruct((CHUNKS, 2, 8, D), BF16),
            in_specs=[hbm, hbm, hbm, vmem, vmem, hbm, hbm, vmem, hbm, hbm, hbm],
            out_specs=hbm,
            scratch_shapes=[
                pltpu.VMEM((ROWS // 8, 8, D), BF16),
                pltpu.VMEM((QD, D), BF16),
                pltpu.VMEM((QD, D), BF16),
                pltpu.VMEM((D, FF), BF16),
                pltpu.VMEM((D, FF), BF16),
                pltpu.VMEM((FF, D), BF16),
                pltpu.VMEM((SLOTS, STACK, SPAN), BF16),
                pltpu.VMEM((SLOTS, STACK, SPAN), BF16),
                pltpu.VMEM((GROUPS, 8, STACK), F32),
                pltpu.VMEM((8, SPAN), F32),
                pltpu.VMEM((8, SPAN), BF16),
                pltpu.VMEM((STACK, QD), BF16),
                pltpu.VMEM((GROUPS, 8, QD), F32),
                pltpu.VMEM((CHUNKS, 2, 8, D), BF16),
                pltpu.VMEM((CHUNKS, 2, 8, D), BF16),
                pltpu.VMEM((CHUNKS, N, 8, OWN), BF16),
                pltpu.VMEM((CHUNKS, N, 8, OWN), BF16),
                pltpu.VMEM((CHUNKS, 2, 8, D), BF16),
                pltpu.VMEM((CHUNKS, 2, 8, D), BF16),
                pltpu.SemaphoreType.DMA((SLOTS, PIECES)),
                pltpu.SemaphoreType.DMA((SLOTS, PIECES)),
                pltpu.SemaphoreType.DMA((6,)),
                pltpu.SemaphoreType.DMA((4,)),
                pltpu.SemaphoreType.DMA((4, CHUNKS)),
                pltpu.SemaphoreType.DMA,
            ],
            compiler_params=pltpu.CompilerParams(
                collective_id=0, has_side_effects=True, vmem_limit_bytes=60 * 2**20
            ),
            name="layer",
        )(
            x.reshape(ROWS // 8, 8, D), stacked(k_cache), stacked(v_cache), turns(), gain_a.reshape(1, D), wq.T, wo,
            gain_m.reshape(1, D), w_gate, w_up, w_down,
        )
        return y.reshape(ROWS, D)

    states, cache, columns, rows_of = P("dp", None), P("dp", None, "tp", None), P(None, "tp"), P("tp", None)
    return jax.shard_map(
        step,
        mesh=mesh,
        in_specs=(states, cache, cache, P(None), columns, rows_of, P(None), columns, columns, rows_of),
        out_specs=states,
        check_vma=False,
    )
```

time: 240 us -> 101 us (0.42)
  waiting for transfers between devices: 132 us -> 0 us
  Pallas kernels: 0 us -> 96.1 us
  matrix products: 82.3 us -> 0 us
  between operations: 13.5 us -> 0.01 us
  other arithmetic: 10.8 us -> 0 us
  local copies, waits for them, and re-layouts: 0.32 us -> 4.36 us
    psum x2 -> x0, waiting for transfers between devices: 132 us -> none  [added(): lax.psum(term.astype(jnp.bfloat16), 'tp').astype(jnp.float32)]
    pallas_call x0 -> x1, Pallas kernels: none -> 96.1 us  [step(): pl.pallas_call(kernel, out_shape=jax.ShapeDtypeStruct((CHUNKS, 2, 8, D),...]
    dot_general x6 -> x0, matrix products: 82.3 us -> none  [the longest x2 70.8 us: einsum(): return jnp.einsum(form, a.astype(jnp.float32), b.astype(jnp.float32))]
    div x1 -> x0, other arithmetic: 5.3 us -> none  [seen_by(): weights = jax.nn.softmax(scores, -1).astype(jnp.bfloat16)]
    convert_element_type x4 -> x0, other arithmetic: 2.71 us -> none  [the longest x1 1.83 us: added(): (t.astype(jnp.float32) + lax.psum(term.astype(jnp.bfloat16), 'tp').astype...]
    reduce_sum x2 -> x0, other arithmetic: 2.58 us -> none  [normed(): scale = lax.rsqrt(jnp.mean(wide * wide, -1, keepdims=True) + 1e-06)]
    reshape x1 -> x2, local copies, waits for them, and re-layouts: 0.09 us -> 2.59 us  [the longest x1 1.3 us: step(): gain_a.reshape(1, D)]
  transfers between devices with their start and end apart: 2 -> 0, of which waited for: 2 -> 0; matrix products, arithmetic and copies ran while one was open for 0% -> 0% of each run, Pallas kernels for 0% -> 0%
where the time goes in v1:
time: 101 us; the launch traced here: 100 us
  Pallas kernels  96.1 us (95%)
  local copies, waits for them, and re-layouts  4.36 us (4%)
    pallas_call x1, Pallas kernels, step(): pl.pallas_call(kernel, out_shape=jax.ShapeDtypeStruct((CHUNKS, 2, 8, D),...  96.1 us

profile of v1, /device:TPU:0, one launch (start us, length us, event | category | flops | bytes accessed | tf_op | source)
XLA Modules:
  0.0 100.5 jit_solution(2442791215114536512)
XLA Ops:
  0.0 1.3 %reshape.21.gain_a_ref = bf16[1,3072]{1,0:T(2,128)(2,1)} reshape(bf16[3072]{0:T(1024)(128)(2,1)} %param.14) | data formatting | bytes 12288 | tf_op jit(solution)/shard_map/reshape | solution.py:314
  1.3 1.3 %reshape.22.gain_m_ref = bf16[1,3072]{1,0:T(2,128)(2,1)} reshape(bf16[3072]{0:T(1024)(128)(2,1)} %param.17) | data formatting | bytes 12288 | tf_op jit(solution)/shard_map/reshape | solution.py:315
  2.6 96.1 %layer.1 = bf16[4,2,8,3072]{3,2,1,0:T(8,128)(2,1)} custom-call(bf16[8,8,3072]{2,1,0:T(8,128)(2,1)} %bitcast.11, bf16[16,768,4096]{2,1,0:T(8,128)(2,1)} %bitcast.2.k_hbm, bf16[16,768,4096]{2,1,0:T(8,128)(2,1)} %bitcast.4.v_hbm, f32[8,192]{1,0:T(8,128)} %constant.2.clone.turn_ref, bf16[1,3072]{1,0:T(2,128)(2,1)} %reshape.21.gain_a_ref, ...), custom_call_target="tpu_custom_call" | custom-call | tf_op jit(solution)/shard_map/layer/pallas_call | solution.py:277
  98.7 1.8 %copy.13 = bf16[64,3072]{1,0:T(8,128)(2,1)} copy(bf16[64,3072]{1,0:T(8,128)(2,1)} %bitcast.9) | data formatting | bytes 786432

commit v2 on v1

v2 whole, which is shorter than its diff:
```python
import functools

import jax
import jax.numpy as jnp
import numpy as np
from jax import lax
from jax.experimental import pallas as pl
from jax.experimental.pallas import tpu as pltpu
from jax.sharding import PartitionSpec as P

HEAD = 96
THETA = 10000

ROWS = 64
D = 3072
SPAN = 4096
QD = 192
FF = 512
GROUP = 4
GROUPS = ROWS // GROUP
STACK = GROUP * QD
SLOTS = 2
LAST_PIECES = 4
BLOCK = 8
BLOCKS = ROWS // BLOCK
BIG = 4
SMALL = 2
STEADY = GROUPS - 2 * SMALL
CHUNKS = STEADY // BIG + 2
N = 16
CHIPS = N // 2
OWN = D // CHIPS

F32, BF16 = jnp.float32, jnp.bfloat16
NT = (((1,), (1,)), ((), ()))
FAR_FIRST = (7, 6, 5, 3, 4, 2, 1)

def dot(a, b):
    return jnp.dot(a, b, preferred_element_type=F32)


def iota(shape, axis):
    return lax.broadcasted_iota(jnp.int32, shape, axis)


def ones_where(keep):
    return jnp.where(keep, 1.0, 0.0).astype(BF16)


def scaled(wide, gain):
    scale = lax.rsqrt(jnp.mean(wide * wide, -1, keepdims=True) + 1e-6)
    return (wide * scale * gain).astype(BF16)


def row_of(ref):
    gain = ref[...].astype(F32)
    return jnp.concatenate([gain[i : i + 1] for i in range(D // 128)], 1)


def any_of(d, values):
    found = d == values[0]
    for v in values[1:]:
        found = found | (d == v)
    return found


def kernel(
    x_hbm, k_hbm, v_hbm, turn_ref, gain_a_ref, wq_hbm, wo_hbm, gain_m_ref, wg_hbm, wu_hbm, wd_hbm,
    y_ref,
    x_v, wq_v, wo_v, wg_v, wu_v, wd_v, k_v, v_v, q_v, fold_v, seen_v,
    p1, p2, r1, r2, hb,
    k_sem, v_sem, w_sem, send_sem, recv_sem,
):
    me = lax.axis_index("tp")
    chip, core = me // 2, me % 2
    columns = pl.ds(pl.multiple_of(chip * OWN, 128), OWN)

    def chip_at(difference):
        return sum((chip // 2**b + (difference >> b)) % 2 * 2**b for b in range(3))

    chips = {difference: chip_at(difference) for difference in FAR_FIRST}

    def k_copy(g):
        slot = lax.rem(g, SLOTS)
        return pltpu.make_async_copy(k_hbm.at[g], k_v.at[slot], k_sem.at[slot])

    def v_copies(g, pieces):
        slot, width = lax.rem(g, SLOTS), SPAN // pieces
        spans = [pl.ds(i * width, width) for i in range(pieces)]
        return [
            (span, pltpu.make_async_copy(v_hbm.at[g, :, span], v_v.at[slot, :, span], v_sem.at[slot, i]))
            for i, span in enumerate(spans)
        ]

    early = [pltpu.make_async_copy(x_hbm, x_v, w_sem.at[0]), pltpu.make_async_copy(wq_hbm, wq_v, w_sem.at[1])]
    late = [
        pltpu.make_async_copy(wo_hbm, wo_v, w_sem.at[2]),
        pltpu.make_async_copy(wg_hbm, wg_v, w_sem.at[3]),
        pltpu.make_async_copy(wu_hbm, wu_v, w_sem.at[4]),
        pltpu.make_async_copy(wd_hbm, wd_v, w_sem.at[5]),
    ]
    for copy in early:
        copy.start()
    for g in range(SLOTS):
        k_copy(g).start()
        for _, copy in v_copies(g, 1):
            copy.start()
    for copy in late:
        copy.start()

    barrier = pltpu.get_barrier_semaphore()
    for p in range(1, N):
        pl.semaphore_signal(barrier, inc=1, device_id={"tp": lax.rem(me + p, N)}, device_id_type=pl.DeviceIdType.MESH)

    for copy in early:
        copy.wait()
    a = scaled(x_v[...].reshape(ROWS, D).astype(F32), row_of(gain_a_ref))
    q = lax.dot_general(a, wq_v[...], NT, preferred_element_type=F32).astype(BF16)
    i, j = iota((QD, QD), 0), iota((QD, QD), 1)
    first = (j < 48) | ((j >= 96) & (j < 144))
    swapped = dot(q, ones_where(((i - j == 48) & first) | ((i - j == -48) & ~first)))
    q = (q.astype(F32) * turn_ref[0:1, :] + swapped * turn_ref[1:2, :]).astype(BF16)
    places = [QD * n for n in range(GROUP)]
    spread = ones_where(any_of(iota((QD, STACK), 1) - iota((QD, STACK), 0), places))
    wide = dot(q, spread).astype(BF16)
    i = iota((2 * ROWS, ROWS), 0)
    wide = dot(ones_where((i >> 3) * GROUP + (i & 3) == iota((2 * ROWS, ROWS), 1)), wide)
    r, c = iota((2 * ROWS, STACK), 0), iota((2 * ROWS, STACK), 1)
    low = (r & 3) * QD + ((r >> 2) & 1) * HEAD
    q_v[...] = jnp.where((c >= low) & (c < low + HEAD), wide, 0.0).reshape(GROUPS, 8, STACK)
    fold_v[...] = ones_where(any_of(iota((STACK, QD), 0) - iota((STACK, QD), 1), places))

    def attend(g, pieces=1, refill=1):
        slot = lax.rem(g, SLOTS)
        k_copy(g).wait()
        s = dot(q_v[g].astype(BF16), k_v[slot]) * HEAD**-0.5
        if refill:
            k_copy(g + SLOTS).start()
        e = jnp.exp(s - jnp.max(s, -1, keepdims=True))
        weights = (e * (1.0 / jnp.sum(e, -1, keepdims=True))).astype(BF16)
        total = jnp.zeros((8, STACK), F32)
        for n, (span, copy) in enumerate(v_copies(g, pieces)):
            copy.wait()
            some = weights[:, n * SPAN // pieces : (n + 1) * SPAN // pieces]
            total += lax.dot_general(some, v_v[slot, :, span], NT, preferred_element_type=F32)
        if refill:
            for _, copy in v_copies(g + SLOTS, refill):
                copy.start()
        r, c = iota((8, STACK), 0), iota((8, STACK), 1)
        low = (r & 3) * QD + (r >> 2) * HEAD
        own = jnp.where((c >= low) & (c < low + HEAD), total, 0.0).astype(BF16)
        seen_v[g] = dot(own, fold_v[...])

    def send(phase, chunk, src, dst, peer):
        pltpu.make_async_remote_copy(
            src_ref=src,
            dst_ref=dst,
            send_sem=send_sem.at[phase],
            recv_sem=recv_sem.at[phase, chunk],
            device_id={"tp": peer},
            device_id_type=pl.DeviceIdType.MESH,
        ).start()

    def of(chunk):
        if isinstance(chunk, int) and chunk >= CHUNKS - 2:
            groups = SMALL
            first = STEADY + (chunk - (CHUNKS - 2)) * SMALL
        else:
            groups = BIG
            first = chunk * BIG
        blocks = groups * GROUP // BLOCK
        start = chunk * blocks if groups == BIG else first * GROUP // BLOCK
        return first, groups, blocks, pl.ds(start, blocks)

    def scatter(phase, chunk, parts, landing):
        rows = of(chunk)[3]
        for difference in FAR_FIRST:
            to = chips[difference]
            theirs = pl.ds(pl.multiple_of(to * OWN, 128), OWN)
            send(phase, chunk, parts.at[rows, :, theirs], landing.at[me, rows], to * 2 + 1)

        @pl.when(core == 0)
        def _():
            send(phase, chunk, parts.at[rows, :, columns], landing.at[me, rows], me + 1)

    def spread_out(phase, chunk, whole):
        block = whole.at[of(chunk)[3], :, columns]
        for difference in FAR_FIRST:
            send(phase, chunk, block, block, chips[difference] * 2)
            send(phase, chunk, block, block, chips[difference] * 2 + 1)
        send(phase, chunk, block, block, me - 1)

    def arrived(phase, chunk, count):
        some = r1.at[pl.ds(0, count), pl.ds(0, of(chunk)[2])]
        pltpu.make_async_copy(some, some, recv_sem.at[phase, chunk]).wait()

    def whole_arrived(phase, chunk):
        @pl.when(core == 1)
        def _():
            arrived(phase, chunk, CHIPS - 1)

        @pl.when(core == 0)
        def _():
            arrived(phase, chunk, CHIPS)

    def finish(phase, chunk, base, parts, landing, whole):
        rows = of(chunk)[3]

        @pl.when(core == 1)
        def _():
            arrived(phase, chunk, N - 1)
            total = parts[rows, :, columns].astype(F32)
            for p in range(1, N):
                total += landing[lax.rem(me + p, N), rows].astype(F32)
            whole[rows, :, columns] = (base[rows, :, columns].astype(F32) + total).astype(BF16)
            spread_out(phase + 1, chunk, whole)

    def project(chunk):
        first, groups, blocks, rows = of(chunk)
        both = seen_v[pl.ds(first, groups)].reshape(8 * groups, QD).astype(BF16)
        shape = (GROUP * groups, 8 * groups)
        i, j = iota(shape, 0), iota(shape, 1)
        seen = dot(ones_where((j >> 3) * GROUP + (j & 3) == i), both).astype(BF16)
        p1[rows] = dot(seen, wo_v[...]).reshape(blocks, BLOCK, D).astype(BF16)
        scatter(0, chunk, p1, r1)

    def finish_h(chunk):
        finish(0, chunk, x_v, p1, r1, hb)

    def mlp(chunk):
        _, _, blocks, rows = of(chunk)
        whole_arrived(1, chunk)
        b = scaled(hb[rows].astype(F32).reshape(blocks * BLOCK, D), row_of(gain_m_ref))
        hidden = (jax.nn.silu(dot(b, wg_v[...])) * dot(b, wu_v[...])).astype(BF16)
        p2[rows] = dot(hidden, wd_v[...]).reshape(blocks, BLOCK, D).astype(BF16)
        scatter(2, chunk, p2, r2)

    def finish_y(chunk):
        finish(2, chunk, hb, p2, r2, y_ref)

    @pl.loop(0, STEADY)
    def _(g):
        attend(g)
        chunk, at = g // BIG, g % BIG

        @pl.when(g == BIG - 1)
        def _():
            for copy in late:
                copy.wait()
            pl.semaphore_wait(barrier, N - 1)

        @pl.when(at == BIG - 1)
        def _():
            project(chunk)

            @pl.when(chunk >= 1)
            def _():
                mlp(chunk - 1)

        @pl.when((at == 1) & (chunk >= 1))
        def _():
            finish_h(chunk - 1)

            @pl.when(chunk >= 2)
            def _():
                finish_y(chunk - 2)

    attend(12)
    attend(13, refill=LAST_PIECES)
    project(3)
    finish_h(2)
    finish_y(1)
    attend(14, refill=0)
    mlp(2)
    finish_h(3)
    attend(15, pieces=LAST_PIECES, refill=0)
    project(4)
    mlp(3)
    finish_y(2)
    finish_h(4)
    finish_y(3)
    mlp(4)
    finish_y(4)
    for chunk in range(CHUNKS):
        whole_arrived(3, chunk)

    def sent(phase, count):
        some = r1.at[pl.ds(0, count)]
        pltpu.make_async_copy(some, some, send_sem.at[phase]).wait()

    @pl.when(core == 1)
    def _():
        for phase, count in ((0, CHIPS - 1), (1, N - 1), (2, CHIPS - 1), (3, N - 1)):
            sent(phase, count)

    @pl.when(core == 0)
    def _():
        for phase in (0, 2):
            sent(phase, CHIPS)


def turns():
    half = HEAD // 2
    angle = (SPAN - 1) * float(THETA) ** (-np.arange(half) / half)
    cos, sin = np.cos(angle), np.sin(angle)
    table = np.zeros((8, QD), np.float32)
    table[0] = np.tile(np.concatenate([cos, cos]), 2)
    table[1] = np.tile(np.concatenate([-sin, sin]), 2)
    return table


def solution(mesh):
    def step(x, k_cache, v_cache, gain_a, wq, wo, gain_m, w_gate, w_up, w_down):
        hbm = pl.BlockSpec(memory_space=pltpu.HBM)
        vmem = pl.BlockSpec(memory_space=pltpu.VMEM)

        def stacked(cache):
            return cache.transpose(0, 2, 3, 1).reshape(GROUPS, STACK, SPAN)

        y = pl.pallas_call(
            kernel,
            out_shape=pltpu.VMEM((BLOCKS, BLOCK, D), BF16),
            in_specs=[hbm, hbm, hbm, vmem, vmem, hbm, hbm, vmem, hbm, hbm, hbm],
            out_specs=vmem,
            scratch_shapes=[
                pltpu.VMEM((BLOCKS, BLOCK, D), BF16),
                pltpu.VMEM((QD, D), BF16),
                pltpu.VMEM((QD, D), BF16),
                pltpu.VMEM((D, FF), BF16),
                pltpu.VMEM((D, FF), BF16),
                pltpu.VMEM((FF, D), BF16),
                pltpu.VMEM((SLOTS, STACK, SPAN), BF16),
                pltpu.VMEM((SLOTS, STACK, SPAN), BF16),
                pltpu.VMEM((GROUPS, 8, STACK), F32),
                pltpu.VMEM((STACK, QD), BF16),
                pltpu.VMEM((GROUPS, 8, QD), F32),
                pltpu.VMEM((BLOCKS, BLOCK, D), BF16),
                pltpu.VMEM((BLOCKS, BLOCK, D), BF16),
                pltpu.VMEM((N, BLOCKS, BLOCK, OWN), BF16),
                pltpu.VMEM((N, BLOCKS, BLOCK, OWN), BF16),
                pltpu.VMEM((BLOCKS, BLOCK, D), BF16),
                pltpu.SemaphoreType.DMA((SLOTS,)),
                pltpu.SemaphoreType.DMA((SLOTS, LAST_PIECES)),
                pltpu.SemaphoreType.DMA((6,)),
                pltpu.SemaphoreType.DMA((4,)),
                pltpu.SemaphoreType.DMA((4, CHUNKS)),
            ],
            compiler_params=pltpu.CompilerParams(
                collective_id=0, has_side_effects=True, vmem_limit_bytes=60 * 2**20
            ),
            name="layer",
        )(
            x.reshape(BLOCKS, BLOCK, D), stacked(k_cache), stacked(v_cache), turns(), gain_a.reshape(D // 128, 128), wq.T, wo,
            gain_m.reshape(D // 128, 128), w_gate, w_up, w_down,
        )
        return y.reshape(ROWS, D)

    states, cache, columns, rows_of = P("dp", None), P("dp", None, "tp", None), P(None, "tp"), P("tp", None)
    return jax.shard_map(
        step,
        mesh=mesh,
        in_specs=(states, cache, cache, P(None), columns, rows_of, P(None), columns, columns, rows_of),
        out_specs=states,
        check_vma=False,
    )
```

time: 101 us -> 89.6 us (0.89)
  Pallas kernels: 96.1 us -> 88.7 us
  local copies, waits for them, and re-layouts: 4.36 us -> 0.75 us
    pallas_call x1, Pallas kernels: 96.1 us -> 88.7 us  [step(): pl.pallas_call(kernel, out_shape=pltpu.VMEM((BLOCKS, BLOCK, D), BF16), in...]
    reshape x2 -> x0, local copies, waits for them, and re-layouts: 2.59 us -> none  [the longest x1 1.3 us: step(): gain_a.reshape(1, D)]
    unnamed x1, local copies, waits for them, and re-layouts: 1.77 us -> 0.75 us
where the time goes in v2:
time: 89.6 us; the launch traced here: 89.4 us
  Pallas kernels  88.7 us (99%)
    pallas_call x1, Pallas kernels, step(): pl.pallas_call(kernel, out_shape=pltpu.VMEM((BLOCKS, BLOCK, D), BF16), in...  88.7 us

profile of v2, /device:TPU:0, one launch (start us, length us, event | category | flops | bytes accessed | tf_op | source)
XLA Modules:
  0.0 89.4 jit_solution(10691094815728700542)
XLA Ops:
  0.0 88.7 %layer.1 = bf16[8,8,3072]{2,1,0:T(8,128)(2,1)S(1)} custom-call(bf16[8,8,3072]{2,1,0:T(8,128)(2,1)} %bitcast.13, bf16[16,768,4096]{2,1,0:T(8,128)(2,1)} %bitcast.2.k_hbm, bf16[16,768,4096]{2,1,0:T(8,128)(2,1)} %bitcast.4.v_hbm, f32[8,192]{1,0:T(8,128)} %constant.2.clone.turn_ref, bf16[24,128]{1,0:T(8,128)(2,1)} %bitcast.14, bf16[192,3072]{1,0:T(8,128)(2,1)} %bitcast.12, ...), custom_call_target="tpu_custom_call" | custom-call | tf_op jit(solution)/shard_map/layer/pallas_call | solution.py:320
  88.7 0.7 copy.13

commit v3 on v2

--- a/solution.py
+++ b/solution.py
@@ -68,7 +68,7 @@
     x_hbm, k_hbm, v_hbm, turn_ref, gain_a_ref, wq_hbm, wo_hbm, gain_m_ref, wg_hbm, wu_hbm, wd_hbm,
     y_ref,
     x_v, wq_v, wo_v, wg_v, wu_v, wd_v, k_v, v_v, q_v, fold_v, seen_v,
-    p1, p2, r1, r2, hb,
+    p1, p2, r1, r2, hb, weights_v, total_v,
     k_sem, v_sem, w_sem, send_sem, recv_sem,
 ):
     me = lax.axis_index("tp")
@@ -80,17 +80,23 @@
 
     chips = {difference: chip_at(difference) for difference in FAR_FIRST}
 
-    def k_copy(g):
-        slot = lax.rem(g, SLOTS)
-        return pltpu.make_async_copy(k_hbm.at[g], k_v.at[slot], k_sem.at[slot])
-
-    def v_copies(g, pieces):
+    def copies(hbm, vmem, sems, g, pieces):
         slot, width = lax.rem(g, SLOTS), SPAN // pieces
         spans = [pl.ds(i * width, width) for i in range(pieces)]
         return [
-            (span, pltpu.make_async_copy(v_hbm.at[g, :, span], v_v.at[slot, :, span], v_sem.at[slot, i]))
+            pltpu.make_async_copy(hbm.at[g, :, span], vmem.at[slot, :, span], sems.at[slot, i])
             for i, span in enumerate(spans)
         ]
+
+    def k_copies(g, pieces=1):
+        return copies(k_hbm, k_v, k_sem, g, pieces)
+
+    def v_copies(g, pieces=1):
+        return copies(v_hbm, v_v, v_sem, g, pieces)
+
+    def start(some):
+        for copy in some:
+            copy.start()
 
     early = [pltpu.make_async_copy(x_hbm, x_v, w_sem.at[0]), pltpu.make_async_copy(wq_hbm, wq_v, w_sem.at[1])]
     late = [
@@ -102,9 +108,7 @@
     for copy in early:
         copy.start()
     for g in range(SLOTS):
-        k_copy(g).start()
-        for _, copy in v_copies(g, 1):
-            copy.start()
+        start(k_copies(g) + v_copies(g))
     for copy in late:
         copy.start()
 
@@ -130,26 +134,40 @@
     q_v[...] = jnp.where((c >= low) & (c < low + HEAD), wide, 0.0).reshape(GROUPS, 8, STACK)
     fold_v[...] = ones_where(any_of(iota((STACK, QD), 0) - iota((STACK, QD), 1), places))
 
-    def attend(g, pieces=1, refill=1):
-        slot = lax.rem(g, SLOTS)
-        k_copy(g).wait()
-        s = dot(q_v[g].astype(BF16), k_v[slot]) * HEAD**-0.5
-        if refill:
-            k_copy(g + SLOTS).start()
-        e = jnp.exp(s - jnp.max(s, -1, keepdims=True))
-        weights = (e * (1.0 / jnp.sum(e, -1, keepdims=True))).astype(BF16)
-        total = jnp.zeros((8, STACK), F32)
-        for n, (span, copy) in enumerate(v_copies(g, pieces)):
-            copy.wait()
-            some = weights[:, n * SPAN // pieces : (n + 1) * SPAN // pieces]
-            total += lax.dot_general(some, v_v[slot, :, span], NT, preferred_element_type=F32)
-        if refill:
-            for _, copy in v_copies(g + SLOTS, refill):
-                copy.start()
+    def keep(g, total):
         r, c = iota((8, STACK), 0), iota((8, STACK), 1)
         low = (r & 3) * QD + (r >> 2) * HEAD
         own = jnp.where((c >= low) & (c < low + HEAD), total, 0.0).astype(BF16)
         seen_v[g] = dot(own, fold_v[...])
+
+    def attend(g, pieces=1, after_keys=None, after_values=None):
+        slot = lax.rem(g, SLOTS)
+
+        @pl.when(me >= 0)
+        def _():
+            k_copies(g)[0].wait()
+            s = dot(q_v[g].astype(BF16), k_v[slot]) * HEAD**-0.5
+            if after_keys:
+                after_keys()
+            e = jnp.exp(s - jnp.max(s, -1, keepdims=True))
+            weights_v[...] = (e * (1.0 / jnp.sum(e, -1, keepdims=True))).astype(BF16)
+
+        for n, copy in enumerate(v_copies(g, pieces)):
+
+            @pl.when(me >= 0)
+            def _():
+                copy.wait()
+                some = pl.ds(n * SPAN // pieces, SPAN // pieces)
+                total = lax.dot_general(weights_v[:, some], v_v[slot, :, some], NT, preferred_element_type=F32)
+                if n:
+                    total += total_v[...]
+                if n == pieces - 1:
+                    keep(g, total)
+                else:
+                    total_v[...] = total
+
+        if after_values:
+            after_values()
 
     def send(phase, chunk, src, dst, peer):
         pltpu.make_async_remote_copy(
@@ -240,7 +258,7 @@
 
     @pl.loop(0, STEADY)
     def _(g):
-        attend(g)
+        attend(g, after_keys=lambda: start(k_copies(g + SLOTS)), after_values=lambda: start(v_copies(g + SLOTS)))
         chunk, at = g // BIG, g % BIG
 
         @pl.when(g == BIG - 1)
@@ -265,21 +283,21 @@
             def _():
                 finish_y(chunk - 2)
 
-    attend(12)
-    attend(13, refill=LAST_PIECES)
+    attend(12, after_keys=lambda: start(k_copies(14)), after_values=lambda: start(v_copies(14, 1)))
+    attend(13, after_keys=lambda: start(k_copies(15)), after_values=lambda: start(v_copies(15, LAST_PIECES)[0:1]))
     project(3)
     finish_h(2)
+    attend(14, after_keys=lambda: start(v_copies(15, LAST_PIECES)[1:2] + v_copies(15, LAST_PIECES)[2:3]), after_values=lambda: start(v_copies(15, LAST_PIECES)[3:4]))
+    attend(15, pieces=LAST_PIECES)
+    project(4)
+    finish_h(3)
+    mlp(2)
+    finish_h(4)
     finish_y(1)
-    attend(14, refill=0)
-    mlp(2)
-    finish_h(3)
-    attend(15, pieces=LAST_PIECES, refill=0)
-    project(4)
     mlp(3)
+    mlp(4)
     finish_y(2)
-    finish_h(4)
     finish_y(3)
-    mlp(4)
     finish_y(4)
     for chunk in range(CHUNKS):
         whole_arrived(3, chunk)
@@ -339,7 +357,9 @@
                 pltpu.VMEM((N, BLOCKS, BLOCK, OWN), BF16),
                 pltpu.VMEM((N, BLOCKS, BLOCK, OWN), BF16),
                 pltpu.VMEM((BLOCKS, BLOCK, D), BF16),
-                pltpu.SemaphoreType.DMA((SLOTS,)),
+                pltpu.VMEM((8, SPAN), BF16),
+                pltpu.VMEM((8, STACK), F32),
+                pltpu.SemaphoreType.DMA((SLOTS, LAST_PIECES)),
                 pltpu.SemaphoreType.DMA((SLOTS, LAST_PIECES)),
                 pltpu.SemaphoreType.DMA((6,)),
                 pltpu.SemaphoreType.DMA((4,)),

time: 89.6 us -> 85.2 us (0.951)
  Pallas kernels: 88.7 us -> 84.2 us
    pallas_call x1, Pallas kernels: 88.7 us -> 84.2 us  [step(): pl.pallas_call(kernel, out_shape=pltpu.VMEM((BLOCKS, BLOCK, D), BF16), in...]
where the time goes in v3:
time: 85.2 us; the launch traced here: 85 us
  Pallas kernels  84.2 us (99%)
    pallas_call x1, Pallas kernels, step(): pl.pallas_call(kernel, out_shape=pltpu.VMEM((BLOCKS, BLOCK, D), BF16), in...  84.2 us

profile of v3, /device:TPU:0, one launch (start us, length us, event | category | flops | bytes accessed | tf_op | source)
XLA Modules:
  0.0 85.0 jit_solution(5288355540763922456)
XLA Ops:
  0.0 84.2 %layer.1 = bf16[8,8,3072]{2,1,0:T(8,128)(2,1)S(1)} custom-call(bf16[8,8,3072]{2,1,0:T(8,128)(2,1)} %bitcast.13, bf16[16,768,4096]{2,1,0:T(8,128)(2,1)} %bitcast.2.k_hbm, bf16[16,768,4096]{2,1,0:T(8,128)(2,1)} %bitcast.4.v_hbm, f32[8,192]{1,0:T(8,128)} %constant.2.clone.turn_ref, bf16[24,128]{1,0:T(8,128)(2,1)} %bitcast.14, bf16[192,3072]{1,0:T(8,128)(2,1)} %bitcast.12, ...), custom_call_target="tpu_custom_call" | custom-call | tf_op jit(solution)/shard_map/layer/pallas_call | solution.py:338
  84.2 0.7 copy.13

commit v4 on v3

--- a/solution.py
+++ b/solution.py
@@ -20,7 +20,7 @@
 GROUPS = ROWS // GROUP
 STACK = GROUP * QD
 SLOTS = 2
-LAST_PIECES = 4
+LAST_PIECES = 2
 BLOCK = 8
 BLOCKS = ROWS // BLOCK
 BIG = 4
@@ -203,9 +203,9 @@
 
     def spread_out(phase, chunk, whole):
         block = whole.at[of(chunk)[3], :, columns]
-        for difference in FAR_FIRST:
-            send(phase, chunk, block, block, chips[difference] * 2)
-            send(phase, chunk, block, block, chips[difference] * 2 + 1)
+        for to in (0, 1):
+            for difference in FAR_FIRST:
+                send(phase, chunk, block, block, chips[difference] * 2 + to)
         send(phase, chunk, block, block, me - 1)
 
     def arrived(phase, chunk, count):
@@ -287,7 +287,7 @@
     attend(13, after_keys=lambda: start(k_copies(15)), after_values=lambda: start(v_copies(15, LAST_PIECES)[0:1]))
     project(3)
     finish_h(2)
-    attend(14, after_keys=lambda: start(v_copies(15, LAST_PIECES)[1:2] + v_copies(15, LAST_PIECES)[2:3]), after_values=lambda: start(v_copies(15, LAST_PIECES)[3:4]))
+    attend(14, after_values=lambda: start(v_copies(15, LAST_PIECES)[1:2]))
     attend(15, pieces=LAST_PIECES)
     project(4)
     finish_h(3)

time: 85.2 us -> 84.1 us (0.987)
  Pallas kernels: 84.2 us -> 83.1 us
    pallas_call x1, Pallas kernels: 84.2 us -> 83.1 us  [step(): pl.pallas_call(kernel, out_shape=pltpu.VMEM((BLOCKS, BLOCK, D), BF16), in...]
where the time goes in v4:
time: 84.1 us; the launch traced here: 83.9 us
  Pallas kernels  83.1 us (99%)
    pallas_call x1, Pallas kernels, step(): pl.pallas_call(kernel, out_shape=pltpu.VMEM((BLOCKS, BLOCK, D), BF16), in...  83.1 us

profile of v4, /device:TPU:0, one launch (start us, length us, event | category | flops | bytes accessed | tf_op | source)
XLA Modules:
  0.0 83.9 jit_solution(14514360906237655995)
XLA Ops:
  0.0 83.1 %layer.1 = bf16[8,8,3072]{2,1,0:T(8,128)(2,1)S(1)} custom-call(bf16[8,8,3072]{2,1,0:T(8,128)(2,1)} %bitcast.13, bf16[16,768,4096]{2,1,0:T(8,128)(2,1)} %bitcast.2.k_hbm, bf16[16,768,4096]{2,1,0:T(8,128)(2,1)} %bitcast.4.v_hbm, f32[8,192]{1,0:T(8,128)} %constant.2.clone.turn_ref, bf16[24,128]{1,0:T(8,128)(2,1)} %bitcast.14, bf16[192,3072]{1,0:T(8,128)(2,1)} %bitcast.12, ...), custom_call_target="tpu_custom_call" | custom-call | tf_op jit(solution)/shard_map/layer/pallas_call | solution.py:338
  83.1 0.7 copy.13
